TPU v7x, 32 devices: a whole 2x2x4 slice. The times are simulated.
32 devices in a mesh: dp: 4 (over x, y), tp: 8 (over z, core).
Axes of the slice: x: 2, y: 2, z: 4, core: 2. Of those that a mesh axis runs over, the one named last changes fastest.
Arguments:
- x: bfloat16 [8192, 2048], P('dp'), parts along dimension 0
- dy: bfloat16 [8192, 2048], P('dp'), parts along dimension 0
- gate: bfloat16 [8192, 6144], P('dp', 'tp'), parts along dimension 0
- up: bfloat16 [8192, 6144], P('dp', 'tp'), parts along dimension 0
- w_gate: bfloat16 [2048, 6144], P(None, 'tp')
- w_up: bfloat16 [2048, 6144], P(None, 'tp')
- w_down: bfloat16 [6144, 2048], P('tp')
Outputs:
- output 1: bfloat16 [8192, 2048], P('dp'), parts along dimension 0
- output 2: bfloat16 [8192, 6144], P('dp', 'tp'), parts along dimension 0
- output 3: bfloat16 [8192, 6144], P('dp', 'tp'), parts along dimension 0
- output 4: bfloat16 [24576, 2048], P(('dp', 'tp')), parts along dimension 0
There are 4 independent parts. A program takes and returns all parts, laid end to end along the dimension named above; an argument that names none is the same for every part.
All inputs are finite; a program needn't handle non-finite values.
Results may differ from a plain program's by a relative error of at most 0.012.
Values are sent between devices in bfloat16 or wider.
A program may use at most 2 GiB of HBM per device.

v0:
```python
import jax
import jax.numpy as jnp
from jax import lax
from jax.sharding import PartitionSpec as P


def act(gate, up):
    return jax.nn.silu(gate) * up


def solution(mesh):
    def step(x, dy, gate, up, w_gate, w_up, w_down):
        hidden, back = jax.vjp(act, gate.astype(jnp.float32), up.astype(jnp.float32))
        d_hidden = jnp.dot(dy, w_down.T, preferred_element_type=jnp.float32)
        d_gate, d_up = (g.astype(jnp.bfloat16) for g in back(d_hidden))
        term = jnp.dot(d_gate, w_gate.T, preferred_element_type=jnp.float32) + jnp.dot(d_up, w_up.T, preferred_element_type=jnp.float32)
        dx = lax.psum(term.astype(jnp.bfloat16), "tp")
        dw_gate = jnp.dot(x.T, d_gate, preferred_element_type=jnp.float32)
        dw_up = jnp.dot(x.T, d_up, preferred_element_type=jnp.float32)
        dw_down = jnp.dot(hidden.astype(jnp.bfloat16).T, dy, preferred_element_type=jnp.float32)
        return dx, *(g.astype(jnp.bfloat16) for g in (dw_gate, dw_up, dw_down))

    tokens, columns, rows = P("dp", None), P(None, "tp"), P("tp", None)
    return jax.shard_map(
        step,
        mesh=mesh,
        in_specs=(tokens, tokens, P("dp", "tp"), P("dp", "tp"), columns, columns, rows),
        out_specs=(tokens, P("dp", "tp"), P("dp", "tp"), P(("dp", "tp"), None)),
        check_vma=False,
    )
```

profile of v0, /device:TPU:0, one launch (start us, length us, event | category | flops | bytes accessed | tf_op | source)
XLA Modules:
  0.0 241.5 jit_solution(1817782558112571582)
XLA Ops:
  7.2 0.0 copy-start
  7.2 0.0 all-reduce.2.cloned.1.call-start
  7.2 14.7 %fusion.6 = (bf16[2048,768]{1,0:T(8,128)(2,1)S(1)}, f32[2048,768]{1,0:T(8,128)}) fusion(bf16[2048,768]{1,0:T(8,128)(2,1)} %param.9, bf16[2048,768]{1,0:T(8,128)(2,1)} %param.10, bf16[2048,2048]{1,0:T(8,128)(2,1)} %param.8, bf16[768,2048]{1,0:T(8,128)(2,1)} %param.13), kind=kOutput, calls=%fused_computation.13 | convolution fusion | flops 6462898176 | bytes 27262976 | tf_op jit(solution)/shard_map/dot_general | solution.py:14
  21.9 0.0 copy-start.2
  21.9 0.0 copy-done
  21.9 9.6 %fusion.11 = f32[2048,2048]{1,0:T(8,128)} fusion(bf16[2048,768]{1,0:T(8,128)(2,1)S(1)} %get-tuple-element.8, bf16[2048,768]{1,0:T(8,128)(2,1)S(1)} %copy-done), kind=kOutput, calls=%fused_computation.21 | convolution fusion | flops 6442450944 | bytes 23068672 | tf_op jit(solution)/shard_map/dot_general | solution.py:16
  31.5 0.0 copy-done.2
  31.5 16.4 %add_convert_fusion = bf16[2048,2048]{1,0:T(8,128)(2,1)} fusion(f32[2048,2048]{1,0:T(8,128)} %fusion.11, bf16[2048,768]{1,0:T(8,128)(2,1)} %param.12, f32[2048,768]{1,0:T(8,128)} %get-tuple-element.9, bf16[2048,768]{1,0:T(8,128)(2,1)} %param.9), kind=kOutput, calls=%fused_computation | convolution fusion | flops 6461849600 | bytes 37748736 | tf_op jit(solution)/shard_map/dot_general | solution.py:16
  47.9 0.0 all-reduce.2.cloned.1.call-update
  48.0 10.1 %fusion.8 = bf16[2048,768]{0,1:T(8,128)(2,1)S(1)} fusion(bf16[2048,768]{1,0:T(8,128)(2,1)} %copy-done.2, bf16[2048,2048]{1,0:T(8,128)(2,1)} %param.7), kind=kOutput, calls=%fused_computation.18 | convolution fusion | flops 6444023808 | bytes 14680064 | tf_op jit(solution)/shard_map/dot_general | solution.py:18
  58.1 2.8 %copy.11 = bf16[2048,768]{1,0:T(8,128)(2,1)} copy(bf16[2048,768]{0,1:T(8,128)(2,1)S(1)} %fusion.8) | data formatting | bytes 6291456
  60.9 12.4 %fusion.9 = bf16[2048,768]{0,1:T(8,128)(2,1)S(1)} fusion(bf16[2048,2048]{1,0:T(8,128)(2,1)} %param.7, f32[2048,768]{1,0:T(8,128)} %get-tuple-element.9, bf16[2048,768]{1,0:T(8,128)(2,1)} %param.9), kind=kOutput, calls=%fused_computation.19 | convolution fusion | flops 6455033856 | bytes 20971520 | tf_op jit(solution)/shard_map/dot_general | solution.py:19
  73.4 2.8 %copy.12 = bf16[2048,768]{1,0:T(8,128)(2,1)} copy(bf16[2048,768]{0,1:T(8,128)(2,1)S(1)} %fusion.9) | data formatting | bytes 6291456
  76.2 0.0 copy-start.1
  76.2 13.3 %convolution_convert_fusion = bf16[768,2048]{1,0:T(8,128)(2,1)} fusion(bf16[2048,2048]{1,0:T(8,128)(2,1)} %param.8, bf16[2048,768]{1,0:T(8,128)(2,1)} %param.10, bf16[2048,768]{1,0:T(8,128)(2,1)} %param.9), kind=kOutput, calls=%fused_computation.15 | convolution fusion | flops 6456606720 | bytes 17825792 | tf_op jit(solution)/shard_map/dot_general | solution.py:20
  89.5 136.7 %all-reduce.2.cloned.1.call-done = bf16[2048,2048]{1,0:T(8,128)(2,1)} async-done(((bf16[2048,2048]{1,0:T(8,128)(2,1)}), bf16[2048,2048]{1,0:T(8,128)(2,1)}) %all-reduce.2.cloned.1.call-update) | async-done | bytes 8388624 | tf_op jit(solution)/shard_map/psum | solution.py:17
  226.2 8.4 %copy.14 = bf16[2048,2048]{1,0:T(8,128)(2,1)} copy(bf16[2048,2048]{1,0:T(8,128)(2,1)} %all-reduce.2.cloned.1.call-done) | data formatting | bytes 16777216
  234.6 0.0 copy-done.1
Async XLA Ops:
  7.2 14.8 %copy-start = (bf16[2048,768]{1,0:T(8,128)(2,1)S(1)}, bf16[2048,768]{1,0:T(8,128)(2,1)}, u32[]{:S(2)}) copy-start(bf16[2048,768]{1,0:T(8,128)(2,1)} %param.11) | copy-start | bytes 9437188
  7.2 219.0 %all-reduce.2.cloned.1.call-start = ((), (), s32[]{:S(2)}) async-start(), calls=%async_computation | async-start | bytes 16777216 | tf_op jit(solution)/shard_map/psum | solution.py:17
  21.9 9.6 %copy-start.2 = (bf16[2048,768]{1,0:T(8,128)(2,1)}, bf16[2048,768]{1,0:T(8,128)(2,1)S(1)}, u32[]{:S(2)}) copy-start(bf16[2048,768]{1,0:T(8,128)(2,1)S(1)} %get-tuple-element.8) | copy-start | bytes 9437188
  76.2 158.5 %copy-start.1 = (bf16[2048,768]{1,0:T(8,128)(2,1)S(1)}, bf16[2048,768]{1,0:T(8,128)(2,1)}, u32[]{:S(2)}) copy-start(bf16[2048,768]{1,0:T(8,128)(2,1)} %param.11) | copy-start | bytes 9437188
Sparse Core Ops, SparseCore 0:
  48.1 178.0 all-reduce.1
where the time goes:
time: 242 us; the launch traced here: 241 us
  waiting for transfers between devices  137 us (57%)
  matrix products  76.6 us (32%)
  between operations  14.1 us (6%)
  local copies, waits for them, and re-layouts  14 us (6%)
    psum x1, waiting for transfers between devices, step(): dx = lax.psum(term.astype(jnp.bfloat16), 'tp')  137 us
    dot_general x1, matrix products, step(): jnp.dot(d_up, w_up.T, preferred_element_type=jnp.float32)  16.4 us
    dot_general x1, matrix products, step(): d_hidden = jnp.dot(dy, w_down.T, preferred_element_type=jnp.float32)  14.7 us
    unnamed x9, local copies, waits for them, and re-layouts  14 us
    dot_general x1, matrix products, step(): jnp.dot(hidden.astype(jnp.bfloat16).T, dy, preferred_element_type=jnp.flo...  13.3 us
    dot_general x1, matrix products, step(): dw_up = jnp.dot(x.T, d_up, preferred_element_type=jnp.float32)  12.4 us
    dot_general x1, matrix products, step(): dw_gate = jnp.dot(x.T, d_gate, preferred_element_type=jnp.float32)  10.1 us
    dot_general x1, matrix products, step(): jnp.dot(d_gate, w_gate.T, preferred_element_type=jnp.float32)  9.59 us
  transfers between devices with their start and end apart: 1, of which 1 were waited for; matrix products, arithmetic and copies ran while one was open for 17% of the time, Pallas kernels for 0%

commit v1 on v0

v1 whole, which is shorter than its diff:
```python
import functools

import jax
import jax.numpy as jnp
from jax import lax
from jax.experimental import pallas as pl
from jax.experimental.pallas import tpu as pltpu
from jax.sharding import PartitionSpec as P

MESH = pl.DeviceIdType.MESH
F32, BF16 = jnp.float32, jnp.bfloat16

ROWS, D, FF = 2048, 2048, 768
RB = 256
CB = 256
HALF = D // 2
NB = ROWS // RB
NC = HALF // CB
CHUNKS = NB * NC
SUB = 2
PIECES = CHUNKS * SUB
PR_ROWS = RB // SUB
SLOTS = 4
HP = FF // 256
LAG_P, LAG_F, LAG_G = 3, 6, 9

NT = (((1,), (1,)), ((), ()))
TN = (((0,), (0,)), ((), ()))


def dot(a, b, dims):
    return lax.dot_general(a, b, dims, preferred_element_type=F32)


def ds(i, n):
    return pl.ds(pl.multiple_of(i * n, n), n)


def kernel(
    x, dy, gate, up, w_gate, w_up, w_down,
    dx, dwg, dwu, dwd,
    dyv, dg, du, hid, own, tb, pr, stage, gv, uv, xv,
    s_dy, s_g, s_u, s_w, s_wd, s_x, s_bs, s_br, s_t, s_in, s_pin, s_f, s_gs, s_gr,
):
    dp, me = lax.axis_index("dp"), lax.axis_index("tp")
    z, c = me // 2, me % 2
    sib = z * 2 + 1 - c
    edge = jnp.logical_or(z == 0, z == 3)
    mid = jnp.logical_not(edge)
    pair = (z + 1 - 2 * (z % 2)) * 2 + c
    across = (3 - z) * 2 + c
    col0 = c * HALF
    sibcol0 = (1 - c) * HALF

    barrier = pltpu.get_barrier_semaphore()
    for d in (sib, pair):
        pl.semaphore_signal(barrier, inc=1, device_id=(dp, d), device_id_type=MESH)

    @pl.when(mid)
    def _():
        pl.semaphore_signal(barrier, inc=1, device_id=(dp, across), device_id_type=MESH)

    def load_dy(b):
        return pltpu.make_async_copy(dy.at[ds(b, RB)], dyv.at[ds(b, RB)], s_dy.at[b])

    def load_g(b):
        return pltpu.make_async_copy(gate.at[ds(b, RB)], gv.at[b % 2], s_g.at[b % 2])

    def load_u(b):
        return pltpu.make_async_copy(up.at[ds(b, RB)], uv.at[b % 2], s_u.at[b % 2])

    def load_wd(h):
        return pltpu.make_async_copy(w_down.at[ds(h, 256)], dwd.at[ds(h, 256)], s_wd.at[h])

    def load_wg(p):
        return pltpu.make_async_copy(w_gate.at[ds(p, CB)], dwg.at[ds(p, CB)], s_w.at[0, p])

    def load_wu(p):
        return pltpu.make_async_copy(w_up.at[ds(p, CB)], dwu.at[ds(p, CB)], s_w.at[1, p])

    def load_x(t):
        return pltpu.make_async_copy(x.at[:, ds(t, 256)], xv.at[t % 2], s_x.at[t % 2])

    load_dy(0).start()
    load_wd(0).start()
    load_g(0).start()
    load_u(0).start()
    for h in range(1, HP):
        load_wd(h).start()
    for n in range(NC):
        for q in ((1 - c) * NC + n, c * NC + n):
            load_wg(q).start()
            load_wu(q).start()
    load_g(1).start()
    load_u(1).start()
    for b in range(1, NB):
        load_dy(b).start()
    load_x(0).start()
    load_x(1).start()

    def d_part(b, h):
        rows, cols = ds(b, RB), ds(h, 256)
        d_hidden = dot(dyv[rows, :], dwd[cols, :], NT)
        g = gv[b % 2, :, cols].astype(F32)
        u = uv[b % 2, :, cols].astype(F32)
        sig = jax.nn.sigmoid(g)
        act = g * sig
        hid[rows, cols] = (act * u).astype(BF16)
        du[rows, cols] = (d_hidden * act).astype(BF16)
        dg[rows, cols] = (d_hidden * u * (sig + act * (1.0 - sig))).astype(BF16)

    def term(b, q):
        rows, cols = ds(b, RB), ds(q, CB)
        return dot(dg[rows, :], dwg[cols, :], NT) + dot(du[rows, :], dwu[cols, :], NT)

    def to_sib(k):
        b, n = k // NC, k % NC
        dst = dx.at[ds(b, RB), ds((1 - c) * NC + n, CB)]
        return pltpu.make_async_remote_copy(
            stage.at[k % SLOTS], dst, s_bs.at[k % SLOTS], s_br.at[k], (dp, sib), MESH
        )

    def spot(s, half):
        k, h = s // SUB, s % SUB
        b, n = k // NC, k % NC
        return ds(b * SUB + h, PR_ROWS), ds(half * NC + n, CB)

    def to_mid(s):
        return pltpu.make_async_remote_copy(tb.at[s], tb.at[s], s_t, s_in.at[s], (dp, pair), MESH)

    def to_across(s):
        return pltpu.make_async_remote_copy(tb.at[s], pr.at[s], s_t, s_pin.at[s], (dp, across), MESH)

    def to_edge(s):
        ref = dx.at[spot(s, c)]
        return pltpu.make_async_remote_copy(ref, ref, s_f, s_in.at[s], (dp, pair), MESH)

    def final_to_sib(s):
        ref = dx.at[spot(s, c)]
        return pltpu.make_async_remote_copy(ref, ref, s_gs, s_gr, (dp, sib), MESH)

    def serve_a(k):
        to_sib(k).wait_recv()
        b, n = k // NC, k % NC
        total = own[k] + dx[ds(b, RB), ds(c * NC + n, CB)].astype(F32)

        @pl.when(edge)
        def _():
            for h in range(SUB):
                s = k * SUB + h
                tb[s] = total[h * PR_ROWS : (h + 1) * PR_ROWS].astype(BF16)
            for h in range(SUB):
                to_mid(k * SUB + h).start()

        @pl.when(mid)
        def _():
            own[k] = total

    def serve_p(s):
        @pl.when(mid)
        def _():
            to_mid(s).wait_recv()
            k, h = s // SUB, s % SUB
            tb[s] = (own[k, ds(h, PR_ROWS), :] + tb[s].astype(F32)).astype(BF16)
            to_across(s).start()

    def serve_f(s):
        @pl.when(mid)
        def _():
            to_across(s).wait_recv()
            dx[spot(s, c)] = (tb[s].astype(F32) + pr[s].astype(F32)).astype(BF16)
            to_edge(s).start()
            final_to_sib(s).start()

    def serve_g(s):
        @pl.when(edge)
        def _():
            to_edge(s).wait_recv()
            final_to_sib(s).start()

    def serve(i):
        for lag, f in ((LAG_P, serve_p), (LAG_F, serve_f), (LAG_G, serve_g)):
            s = i - lag
            pl.when(jnp.logical_and(s >= 0, s < PIECES))(functools.partial(f, s))

    def serve_all(i):
        serve_p(i - LAG_P)
        serve_f(i - LAG_F)
        serve_g(i - LAG_G)

    load_dy(0).wait()
    load_g(0).wait()
    load_u(0).wait()
    for h in range(HP):
        load_wd(h).wait()
        d_part(0, h)
    load_g(2).start()
    load_u(2).start()

    @pl.when(edge)
    def _():
        pl.semaphore_wait(barrier, 2)

    @pl.when(mid)
    def _():
        pl.semaphore_wait(barrier, 3)

    def step1(i, _):
        b, n = i // NC, i % NC
        qs, qo = (1 - c) * NC + n, c * NC + n

        @pl.when(b == 0)
        def _():
            load_wg(qs).wait()
            load_wu(qs).wait()

        @pl.when(i >= SLOTS)
        def _():
            to_sib(i - SLOTS).wait_send()

        stage[i % SLOTS] = term(b, qs).astype(BF16)
        to_sib(i).start()

        @pl.when(i >= 1)
        def _():
            serve_a(i - 1)

        @pl.when(b == 0)
        def _():
            load_wg(qo).wait()
            load_wu(qo).wait()

        own[i] = term(b, qo)
        serve(i)

        @pl.when(jnp.logical_and(n == 0, b < NB - 1))
        def _():
            load_dy(b + 1).wait()
            load_g(b + 1).wait()
            load_u(b + 1).wait()

        @pl.when(jnp.logical_and(n < HP, b < NB - 1))
        def _():
            d_part(b + 1, n)

        @pl.when(jnp.logical_and(n == NC - 1, b < NB - 3))
        def _():
            load_g(b + 3).start()
            load_u(b + 3).start()

        return 0

    lax.fori_loop(0, CHUNKS, step1, 0)
    serve_a(CHUNKS - 1)

    def step2(t, _):
        load_x(t).wait()
        rows = ds(t, 256)
        dwg[rows, :] = dot(xv[t % 2], dg[...], TN).astype(BF16)
        serve_all(CHUNKS + 2 * t)
        dwu[rows, :] = dot(xv[t % 2], du[...], TN).astype(BF16)

        @pl.when(t < D // 256 - 2)
        def _():
            load_x(t + 2).start()

        serve_all(CHUNKS + 2 * t + 1)
        return 0

    lax.fori_loop(0, D // 256, step2, 0)
    base = CHUNKS + 2 * (D // 256)

    def step3(i, _):
        rows, cols = ds(i // 4, 256), ds(i % 4, 512)
        dwd[rows, cols] = dot(hid[:, rows], dyv[:, cols], TN).astype(BF16)
        serve_all(base + i)
        return 0

    lax.fori_loop(0, HP * 4, step3, 0)
    base = base + HP * 4

    def step4(i, _):
        serve(i)
        return 0

    lax.fori_loop(base, PIECES + LAG_G, step4, 0)

    for k in range(SLOTS):
        to_sib(CHUNKS - SLOTS + k).wait_send()
    other = dx.at[:, ds(1 - c, HALF)]
    mine = dx.at[:, ds(c, HALF)]
    pltpu.make_async_copy(tb, tb, s_t).wait()
    pltpu.make_async_copy(mine, mine, s_gs).wait()
    pltpu.make_async_copy(other, other, s_gr).wait()

    @pl.when(mid)
    def _():
        pltpu.make_async_copy(mine, mine, s_f).wait()


def writer(a, b, c, d, oa, ob, oc, od, sems):
    copies = [pltpu.make_async_copy(s, t, sems.at[i]) for i, (s, t) in enumerate(((a, oa), (b, ob), (c, oc), (d, od)))]
    for copy in copies:
        copy.start()
    for copy in copies:
        copy.wait()


def solution(mesh):
    shapes = ((ROWS, D), (D, FF), (D, FF), (FF, D))

    def step(*args):
        dma = pltpu.SemaphoreType.DMA
        parts = pl.pallas_call(
            kernel,
            out_shape=[pltpu.VMEM(s, BF16) for s in shapes],
            in_specs=[pl.BlockSpec(memory_space=pl.ANY)] * 7,
            out_specs=[pl.BlockSpec(memory_space=pltpu.VMEM)] * 4,
            scratch_shapes=[
                pltpu.VMEM((ROWS, D), BF16),
                pltpu.VMEM((ROWS, FF), BF16),
                pltpu.VMEM((ROWS, FF), BF16),
                pltpu.VMEM((ROWS, FF), BF16),
                pltpu.VMEM((CHUNKS, RB, CB), F32),
                pltpu.VMEM((PIECES, PR_ROWS, CB), BF16),
                pltpu.VMEM((PIECES, PR_ROWS, CB), BF16),
                pltpu.VMEM((SLOTS, RB, CB), BF16),
                pltpu.VMEM((2, RB, FF), BF16),
                pltpu.VMEM((2, RB, FF), BF16),
                pltpu.VMEM((2, ROWS, 256), BF16),
                dma((NB,)),
                dma((2,)),
                dma((2,)),
                dma((2, 2 * NC)),
                dma((HP,)),
                dma((2,)),
                dma((SLOTS,)),
                dma((CHUNKS,)),
                dma,
                dma((PIECES,)),
                dma((PIECES,)),
                dma,
                dma,
                dma,
            ],
            compiler_params=pltpu.CompilerParams(
                collective_id=0, has_side_effects=True, vmem_limit_bytes=44 * 1024 * 1024
            ),
        )(*args)
        return pl.pallas_call(
            writer,
            out_shape=[jax.ShapeDtypeStruct(s, BF16) for s in shapes],
            in_specs=[pl.BlockSpec(memory_space=pltpu.VMEM)] * 4,
            out_specs=[pl.BlockSpec(memory_space=pl.ANY)] * 4,
            scratch_shapes=[pltpu.SemaphoreType.DMA((4,))],
            compiler_params=pltpu.CompilerParams(vmem_limit_bytes=1024 * 1024),
        )(*parts)

    tokens, columns, rows = P("dp", None), P(None, "tp"), P("tp", None)
    return jax.shard_map(
        step,
        mesh=mesh,
        in_specs=(tokens, tokens, P("dp", "tp"), P("dp", "tp"), columns, columns, rows),
        out_specs=(tokens, P("dp", "tp"), P("dp", "tp"), P(("dp", "tp"), None)),
        check_vma=False,
    )
```

time: 242 us -> 130 us (0.54)
  waiting for transfers between devices: 137 us -> 0 us
  Pallas kernels: 0 us -> 129 us
  matrix products: 76.6 us -> 0 us
  local copies, waits for them, and re-layouts: 14 us -> 0 us
  between operations: 14.1 us -> 0.64 us
    psum x1 -> x0, waiting for transfers between devices: 137 us -> none  [step(): dx = lax.psum(term.astype(jnp.bfloat16), 'tp')]
    pallas_call x0 -> x2, Pallas kernels: none -> 129 us  [the longest x1 123 us: step(): pl.pallas_call(kernel, out_shape=[pltpu.VMEM(s, BF16) for s in shapes], i...]
    dot_general x6 -> x0, matrix products: 76.6 us -> none  [the longest x1 16.4 us: step(): jnp.dot(d_up, w_up.T, preferred_element_type=jnp.float32)]
    unnamed x9 -> x0, local copies, waits for them, and re-layouts: 14 us -> none
  transfers between devices with their start and end apart: 1 -> 0, of which waited for: 1 -> 0; matrix products, arithmetic and copies ran while one was open for 17% -> 0% of each run, Pallas kernels for 0% -> 0%
where the time goes in v1:
time: 130 us
  Pallas kernels  129 us (99%)
    pallas_call x1, Pallas kernels, step(): pl.pallas_call(kernel, out_shape=[pltpu.VMEM(s, BF16) for s in shapes], i...  123 us
    pallas_call x1, Pallas kernels, step(): pl.pallas_call(writer, out_shape=[jax.ShapeDtypeStruct(s, BF16) for s in...  6.35 us

profile of v1, /device:TPU:0, one launch (start us, length us, event | category | flops | bytes accessed | tf_op | source)
XLA Modules:
  0.0 129.9 jit_solution(2851234512726549386)
XLA Ops:
  0.6 122.9 %shard_map.102 = (bf16[2048,2048]{1,0:T(8,128)(2,1)S(1)}, bf16[2048,768]{1,0:T(8,128)(2,1)S(1)}, bf16[2048,768]{1,0:T(8,128)(2,1)S(1)}, bf16[768,2048]{1,0:T(8,128)(2,1)S(1)}) custom-call(bf16[2048,2048]{1,0:T(8,128)(2,1)} %x.1, bf16[2048,2048]{1,0:T(8,128)(2,1)} %dy.1, bf16[2048,768]{1,0:T(8,128)(2,1)} %gate.1, bf16[2048,768]{1,0:T(8,128)(2,1)} %up.1, ...), custom_call_target="tpu_custom_call" | custom-call | tf_op jit(solution)/shard_map/pallas_call | solution.py:314
  123.6 6.4 %shard_map.103 = (bf16[2048,2048]{1,0:T(8,128)(2,1)}, bf16[2048,768]{1,0:T(8,128)(2,1)}, bf16[2048,768]{1,0:T(8,128)(2,1)}, bf16[768,2048]{1,0:T(8,128)(2,1)}) custom-call(bf16[2048,2048]{1,0:T(8,128)(2,1)S(1)} %get-tuple-element.8.a, bf16[2048,768]{1,0:T(8,128)(2,1)S(1)} %get-tuple-element.9.b, bf16[2048,768]{1,0:T(8,128)(2,1)S(1)} %get-tuple-element.10.c, ...), custom_call_target="tpu_custom_call" | custom-call | tf_op jit(solution)/shard_map/pallas_call | solution.py:350

commit v2 on v1

--- a/solution.py
+++ b/solution.py
@@ -23,6 +23,7 @@
 SLOTS = 4
 HP = FF // 256
 LAG_P, LAG_F, LAG_G = 3, 6, 9
+PER_BLOCK = NC + 1
 
 NT = (((1,), (1,)), ((), ()))
 TN = (((0,), (0,)), ((), ()))
@@ -30,6 +31,14 @@
 
 def dot(a, b, dims):
     return lax.dot_general(a, b, dims, preferred_element_type=F32)
+
+
+def div(a, n):
+    return lax.div(a, jnp.int32(n)) if isinstance(a, jax.Array) else a // n
+
+
+def rem(a, n):
+    return lax.rem(a, jnp.int32(n)) if isinstance(a, jax.Array) else a % n
 
 
 def ds(i, n):
@@ -39,15 +48,15 @@
 def kernel(
     x, dy, gate, up, w_gate, w_up, w_down,
     dx, dwg, dwu, dwd,
-    dyv, dg, du, hid, own, tb, pr, stage, gv, uv, xv,
+    dyv, dgu, hid, own, tb, pr, stage, gv, uv, xv,
     s_dy, s_g, s_u, s_w, s_wd, s_x, s_bs, s_br, s_t, s_in, s_pin, s_f, s_gs, s_gr,
 ):
     dp, me = lax.axis_index("dp"), lax.axis_index("tp")
-    z, c = me // 2, me % 2
+    z, c = div(me, 2), rem(me, 2)
     sib = z * 2 + 1 - c
     edge = jnp.logical_or(z == 0, z == 3)
     mid = jnp.logical_not(edge)
-    pair = (z + 1 - 2 * (z % 2)) * 2 + c
+    pair = (z + 1 - 2 * rem(z, 2)) * 2 + c
     across = (3 - z) * 2 + c
     col0 = c * HALF
     sibcol0 = (1 - c) * HALF
@@ -64,10 +73,10 @@
         return pltpu.make_async_copy(dy.at[ds(b, RB)], dyv.at[ds(b, RB)], s_dy.at[b])
 
     def load_g(b):
-        return pltpu.make_async_copy(gate.at[ds(b, RB)], gv.at[b % 2], s_g.at[b % 2])
+        return pltpu.make_async_copy(gate.at[ds(b, RB)], gv.at[rem(b, 2)], s_g.at[rem(b, 2)])
 
     def load_u(b):
-        return pltpu.make_async_copy(up.at[ds(b, RB)], uv.at[b % 2], s_u.at[b % 2])
+        return pltpu.make_async_copy(up.at[ds(b, RB)], uv.at[rem(b, 2)], s_u.at[rem(b, 2)])
 
     def load_wd(h):
         return pltpu.make_async_copy(w_down.at[ds(h, 256)], dwd.at[ds(h, 256)], s_wd.at[h])
@@ -79,50 +88,49 @@
         return pltpu.make_async_copy(w_up.at[ds(p, CB)], dwu.at[ds(p, CB)], s_w.at[1, p])
 
     def load_x(t):
-        return pltpu.make_async_copy(x.at[:, ds(t, 256)], xv.at[t % 2], s_x.at[t % 2])
-
-    load_dy(0).start()
-    load_wd(0).start()
-    load_g(0).start()
-    load_u(0).start()
-    for h in range(1, HP):
-        load_wd(h).start()
-    for n in range(NC):
+        return pltpu.make_async_copy(x.at[:, ds(t, 256)], xv.at[rem(t, 2)], s_x.at[rem(t, 2)])
+
+    def load_w(n):
         for q in ((1 - c) * NC + n, c * NC + n):
             load_wg(q).start()
             load_wu(q).start()
-    load_g(1).start()
-    load_u(1).start()
-    for b in range(1, NB):
+
+    def load_rows(b):
         load_dy(b).start()
-    load_x(0).start()
-    load_x(1).start()
+        load_g(b).start()
+        load_u(b).start()
+
+    load_wd(0).start()
+    load_rows(0)
+    load_wd(1).start()
+    load_wd(2).start()
+    load_w(0)
 
     def d_part(b, h):
         rows, cols = ds(b, RB), ds(h, 256)
         d_hidden = dot(dyv[rows, :], dwd[cols, :], NT)
-        g = gv[b % 2, :, cols].astype(F32)
-        u = uv[b % 2, :, cols].astype(F32)
+        g = gv[rem(b, 2), :, cols].astype(F32)
+        u = uv[rem(b, 2), :, cols].astype(F32)
         sig = jax.nn.sigmoid(g)
         act = g * sig
         hid[rows, cols] = (act * u).astype(BF16)
-        du[rows, cols] = (d_hidden * act).astype(BF16)
-        dg[rows, cols] = (d_hidden * u * (sig + act * (1.0 - sig))).astype(BF16)
+        dgu[rows, ds(HP + h, 256)] = (d_hidden * act).astype(BF16)
+        dgu[rows, cols] = (d_hidden * u * (sig + act * (1.0 - sig))).astype(BF16)
 
     def term(b, q):
         rows, cols = ds(b, RB), ds(q, CB)
-        return dot(dg[rows, :], dwg[cols, :], NT) + dot(du[rows, :], dwu[cols, :], NT)
+        return dot(dgu[rows, :FF], dwg[cols, :], NT) + dot(dgu[rows, FF:], dwu[cols, :], NT)
 
     def to_sib(k):
-        b, n = k // NC, k % NC
+        b, n = div(k, NC), rem(k, NC)
         dst = dx.at[ds(b, RB), ds((1 - c) * NC + n, CB)]
         return pltpu.make_async_remote_copy(
-            stage.at[k % SLOTS], dst, s_bs.at[k % SLOTS], s_br.at[k], (dp, sib), MESH
+            stage.at[rem(k, SLOTS)], dst, s_bs.at[rem(k, SLOTS)], s_br.at[k], (dp, sib), MESH
         )
 
     def spot(s, half):
-        k, h = s // SUB, s % SUB
-        b, n = k // NC, k % NC
+        k, h = div(s, SUB), rem(s, SUB)
+        b, n = div(k, NC), rem(k, NC)
         return ds(b * SUB + h, PR_ROWS), ds(half * NC + n, CB)
 
     def to_mid(s):
@@ -141,7 +149,7 @@
 
     def serve_a(k):
         to_sib(k).wait_recv()
-        b, n = k // NC, k % NC
+        b, n = div(k, NC), rem(k, NC)
         total = own[k] + dx[ds(b, RB), ds(c * NC + n, CB)].astype(F32)
 
         @pl.when(edge)
@@ -160,7 +168,7 @@
         @pl.when(mid)
         def _():
             to_mid(s).wait_recv()
-            k, h = s // SUB, s % SUB
+            k, h = div(s, SUB), rem(s, SUB)
             tb[s] = (own[k, ds(h, PR_ROWS), :] + tb[s].astype(F32)).astype(BF16)
             to_across(s).start()
 
@@ -182,20 +190,17 @@
         for lag, f in ((LAG_P, serve_p), (LAG_F, serve_f), (LAG_G, serve_g)):
             s = i - lag
             pl.when(jnp.logical_and(s >= 0, s < PIECES))(functools.partial(f, s))
-
-    def serve_all(i):
-        serve_p(i - LAG_P)
-        serve_f(i - LAG_F)
-        serve_g(i - LAG_G)
 
     load_dy(0).wait()
     load_g(0).wait()
     load_u(0).wait()
     for h in range(HP):
         load_wd(h).wait()
+        if h == HP - 1:
+            for n in range(1, NC):
+                load_w(n)
+            load_rows(1)
         d_part(0, h)
-    load_g(2).start()
-    load_u(2).start()
 
     @pl.when(edge)
     def _():
@@ -206,47 +211,50 @@
         pl.semaphore_wait(barrier, 3)
 
     def step1(i, _):
-        b, n = i // NC, i % NC
+        b, n = div(i, NC), rem(i, NC)
         qs, qo = (1 - c) * NC + n, c * NC + n
 
         @pl.when(b == 0)
         def _():
-            load_wg(qs).wait()
-            load_wu(qs).wait()
+            for q in (qs, qo):
+                load_wg(q).wait()
+                load_wu(q).wait()
 
         @pl.when(i >= SLOTS)
         def _():
             to_sib(i - SLOTS).wait_send()
 
-        stage[i % SLOTS] = term(b, qs).astype(BF16)
+        theirs, ours = term(b, qs), term(b, qo)
+        stage[rem(i, SLOTS)] = theirs.astype(BF16)
+        own[i] = ours
         to_sib(i).start()
 
         @pl.when(i >= 1)
         def _():
             serve_a(i - 1)
 
-        @pl.when(b == 0)
-        def _():
-            load_wg(qo).wait()
-            load_wu(qo).wait()
-
-        own[i] = term(b, qo)
-        serve(i)
-
-        @pl.when(jnp.logical_and(n == 0, b < NB - 1))
+        serve(b * PER_BLOCK + n)
+
+        @pl.when(jnp.logical_and(n == 1, b < NB - 1))
         def _():
             load_dy(b + 1).wait()
             load_g(b + 1).wait()
             load_u(b + 1).wait()
 
-        @pl.when(jnp.logical_and(n < HP, b < NB - 1))
-        def _():
-            d_part(b + 1, n)
-
-        @pl.when(jnp.logical_and(n == NC - 1, b < NB - 3))
-        def _():
-            load_g(b + 3).start()
-            load_u(b + 3).start()
+            @pl.when(b < NB - 2)
+            def _():
+                load_rows(b + 2)
+
+        @pl.when(jnp.logical_and(n >= 1, b < NB - 1))
+        def _():
+            d_part(b + 1, n - 1)
+
+        pl.when(n == NC - 1)(functools.partial(serve, b * PER_BLOCK + NC))
+
+        @pl.when(i == CHUNKS - 2)
+        def _():
+            load_x(0).start()
+            load_x(1).start()
 
         return 0
 
@@ -256,28 +264,36 @@
     def step2(t, _):
         load_x(t).wait()
         rows = ds(t, 256)
-        dwg[rows, :] = dot(xv[t % 2], dg[...], TN).astype(BF16)
-        serve_all(CHUNKS + 2 * t)
-        dwu[rows, :] = dot(xv[t % 2], du[...], TN).astype(BF16)
-
-        @pl.when(t < D // 256 - 2)
-        def _():
-            load_x(t + 2).start()
-
-        serve_all(CHUNKS + 2 * t + 1)
+        for q in range(3):
+            part = dot(xv[rem(t, 2)], dgu[:, q * 512 : (q + 1) * 512], TN).astype(BF16)
+            if q == 0:
+                dwg[rows, :512] = part
+            elif q == 1:
+                dwg[rows, 512:] = part[:, :256]
+                dwu[rows, :256] = part[:, 256:]
+            else:
+                dwu[rows, 256:] = part
+
+                @pl.when(t < D // 256 - 2)
+                def _():
+                    load_x(t + 2).start()
+
+            if q > 0:
+                serve(NB * PER_BLOCK + 2 * t + q - 1)
         return 0
 
     lax.fori_loop(0, D // 256, step2, 0)
-    base = CHUNKS + 2 * (D // 256)
+    base = NB * PER_BLOCK + 2 * (D // 256)
 
     def step3(i, _):
-        rows, cols = ds(i // 4, 256), ds(i % 4, 512)
+        q, h = div(i, HP), rem(i, HP)
+        rows, cols = ds(h, 256), ds(q, 512)
         dwd[rows, cols] = dot(hid[:, rows], dyv[:, cols], TN).astype(BF16)
-        serve_all(base + i)
+        pl.when(h > 0)(functools.partial(serve, base + q * (HP - 1) + h - 1))
         return 0
 
     lax.fori_loop(0, HP * 4, step3, 0)
-    base = base + HP * 4
+    base = base + (HP - 1) * 4
 
     def step4(i, _):
         serve(i)
@@ -318,8 +334,7 @@
             out_specs=[pl.BlockSpec(memory_space=pltpu.VMEM)] * 4,
             scratch_shapes=[
                 pltpu.VMEM((ROWS, D), BF16),
-                pltpu.VMEM((ROWS, FF), BF16),
-                pltpu.VMEM((ROWS, FF), BF16),
+                pltpu.VMEM((ROWS, 2 * FF), BF16),
                 pltpu.VMEM((ROWS, FF), BF16),
                 pltpu.VMEM((CHUNKS, RB, CB), F32),
                 pltpu.VMEM((PIECES, PR_ROWS, CB), BF16),

time: 130 us -> 119 us (0.915)
  Pallas kernels: 129 us -> 119 us
    pallas_call x1, Pallas kernels: 123 us -> 112 us  [step(): pl.pallas_call(kernel, out_shape=[pltpu.VMEM(s, BF16) for s in shapes], i...]
where the time goes in v2:
time: 119 us
  Pallas kernels  119 us (100%)
    pallas_call x1, Pallas kernels, step(): pl.pallas_call(kernel, out_shape=[pltpu.VMEM(s, BF16) for s in shapes], i...  112 us
    pallas_call x1, Pallas kernels, step(): pl.pallas_call(writer, out_shape=[jax.ShapeDtypeStruct(s, BF16) for s in...  6.35 us

profile of v2, /device:TPU:0, one launch (start us, length us, event | category | flops | bytes accessed | tf_op | source)
XLA Modules:
  0.0 119.2 jit_solution(18076617522394927257)
XLA Ops:
  0.6 112.2 %shard_map.102 = (bf16[2048,2048]{1,0:T(8,128)(2,1)S(1)}, bf16[2048,768]{1,0:T(8,128)(2,1)S(1)}, bf16[2048,768]{1,0:T(8,128)(2,1)S(1)}, bf16[768,2048]{1,0:T(8,128)(2,1)S(1)}) custom-call(bf16[2048,2048]{1,0:T(8,128)(2,1)} %x.1, bf16[2048,2048]{1,0:T(8,128)(2,1)} %dy.1, bf16[2048,768]{1,0:T(8,128)(2,1)} %gate.1, bf16[2048,768]{1,0:T(8,128)(2,1)} %up.1, ...), custom_call_target="tpu_custom_call" | custom-call | tf_op jit(solution)/shard_map/pallas_call | solution.py:330
  112.9 6.4 %shard_map.103 = (bf16[2048,2048]{1,0:T(8,128)(2,1)}, bf16[2048,768]{1,0:T(8,128)(2,1)}, bf16[2048,768]{1,0:T(8,128)(2,1)}, bf16[768,2048]{1,0:T(8,128)(2,1)}) custom-call(bf16[2048,2048]{1,0:T(8,128)(2,1)S(1)} %get-tuple-element.8.a, bf16[2048,768]{1,0:T(8,128)(2,1)S(1)} %get-tuple-element.9.b, bf16[2048,768]{1,0:T(8,128)(2,1)S(1)} %get-tuple-element.10.c, ...), custom_call_target="tpu_custom_call" | custom-call | tf_op jit(solution)/shard_map/pallas_call | solution.py:365

commit v3 on v2

--- a/solution.py
+++ b/solution.py
@@ -12,17 +12,17 @@
 
 ROWS, D, FF = 2048, 2048, 768
 RB = 256
-CB = 256
-HALF = D // 2
+CB = 512
 NB = ROWS // RB
-NC = HALF // CB
+NC = D // CB
 CHUNKS = NB * NC
 SUB = 2
 PIECES = CHUNKS * SUB
 PR_ROWS = RB // SUB
 SLOTS = 4
+DEPTH = 16
 HP = FF // 256
-LAG_P, LAG_F, LAG_G = 3, 6, 9
+LAG_P, LAG_F, LAG_G = 4, 8, 12
 PER_BLOCK = NC + 1
 
 NT = (((1,), (1,)), ((), ()))
@@ -48,8 +48,8 @@
 def kernel(
     x, dy, gate, up, w_gate, w_up, w_down,
     dx, dwg, dwu, dwd,
-    dyv, dgu, hid, own, tb, pr, stage, gv, uv, xv,
-    s_dy, s_g, s_u, s_w, s_wd, s_x, s_bs, s_br, s_t, s_in, s_pin, s_f, s_gs, s_gr,
+    dyv, dgu, hid, own, tb, stage, gv, uv, xv,
+    s_dy, s_g, s_u, s_w, s_wd, s_x, s_bs, s_br, s_t, s_in, s_pl, s_f, s_gs, s_gr,
 ):
     dp, me = lax.axis_index("dp"), lax.axis_index("tp")
     z, c = div(me, 2), rem(me, 2)
@@ -57,17 +57,8 @@
     edge = jnp.logical_or(z == 0, z == 3)
     mid = jnp.logical_not(edge)
     pair = (z + 1 - 2 * rem(z, 2)) * 2 + c
-    across = (3 - z) * 2 + c
-    col0 = c * HALF
-    sibcol0 = (1 - c) * HALF
-
-    barrier = pltpu.get_barrier_semaphore()
-    for d in (sib, pair):
-        pl.semaphore_signal(barrier, inc=1, device_id=(dp, d), device_id_type=MESH)
-
-    @pl.when(mid)
-    def _():
-        pl.semaphore_signal(barrier, inc=1, device_id=(dp, across), device_id_type=MESH)
+    across = (3 - z) * 2 + 1 - c
+    adds, ends = c == 1, c == 0
 
     def load_dy(b):
         return pltpu.make_async_copy(dy.at[ds(b, RB)], dyv.at[ds(b, RB)], s_dy.at[b])
@@ -91,9 +82,8 @@
         return pltpu.make_async_copy(x.at[:, ds(t, 256)], xv.at[rem(t, 2)], s_x.at[rem(t, 2)])
 
     def load_w(n):
-        for q in ((1 - c) * NC + n, c * NC + n):
-            load_wg(q).start()
-            load_wu(q).start()
+        load_wg(n).start()
+        load_wu(n).start()
 
     def load_rows(b):
         load_dy(b).start()
@@ -105,6 +95,15 @@
     load_wd(1).start()
     load_wd(2).start()
     load_w(0)
+
+    barrier = pltpu.get_barrier_semaphore()
+    for d in (sib, pair):
+        pl.semaphore_signal(barrier, inc=1, device_id=(dp, d), device_id_type=MESH)
+
+    @pl.when(mid)
+    def _():
+        pl.semaphore_signal(barrier, inc=1, device_id=(dp, across), device_id_type=MESH)
+
 
     def d_part(b, h):
         rows, cols = ds(b, RB), ds(h, 256)
@@ -117,71 +116,86 @@
         dgu[rows, ds(HP + h, 256)] = (d_hidden * act).astype(BF16)
         dgu[rows, cols] = (d_hidden * u * (sig + act * (1.0 - sig))).astype(BF16)
 
-    def term(b, q):
-        rows, cols = ds(b, RB), ds(q, CB)
+    def term(k):
+        rows, cols = ds(div(k, NC), RB), ds(rem(k, NC), CB)
         return dot(dgu[rows, :FF], dwg[cols, :], NT) + dot(dgu[rows, FF:], dwu[cols, :], NT)
 
+    def remote(src, dst, send, recv, device):
+        return pltpu.make_async_remote_copy(src, dst, send, recv, (dp, device), MESH)
+
+    def tile(k):
+        return ds(div(k, NC), RB), ds(rem(k, NC), CB)
+
+    def spot(s):
+        k, h = div(s, SUB), rem(s, SUB)
+        return ds(div(k, NC) * SUB + h, PR_ROWS), ds(rem(k, NC), CB)
+
     def to_sib(k):
-        b, n = div(k, NC), rem(k, NC)
-        dst = dx.at[ds(b, RB), ds((1 - c) * NC + n, CB)]
-        return pltpu.make_async_remote_copy(
-            stage.at[rem(k, SLOTS)], dst, s_bs.at[rem(k, SLOTS)], s_br.at[k], (dp, sib), MESH
-        )
-
-    def spot(s, half):
-        k, h = div(s, SUB), rem(s, SUB)
-        b, n = div(k, NC), rem(k, NC)
-        return ds(b * SUB + h, PR_ROWS), ds(half * NC + n, CB)
+        q = rem(k, SLOTS)
+        return remote(stage.at[q], dx.at[tile(k)], s_bs.at[q], s_br.at[k], sib)
 
     def to_mid(s):
-        return pltpu.make_async_remote_copy(tb.at[s], tb.at[s], s_t, s_in.at[s], (dp, pair), MESH)
+        return remote(tb.at[s], tb.at[s], s_t, s_in.at[s], pair)
 
     def to_across(s):
-        return pltpu.make_async_remote_copy(tb.at[s], pr.at[s], s_t, s_pin.at[s], (dp, across), MESH)
+        return remote(tb.at[s], tb.at[s], s_t, s_in.at[s], across)
+
+    def part_to_sib(s):
+        return remote(tb.at[s], dx.at[spot(s)], s_gs, s_pl.at[s], sib)
 
     def to_edge(s):
-        ref = dx.at[spot(s, c)]
-        return pltpu.make_async_remote_copy(ref, ref, s_f, s_in.at[s], (dp, pair), MESH)
+        ref = dx.at[spot(s)]
+        return remote(ref, ref, s_f, s_in.at[s], pair)
 
     def final_to_sib(s):
-        ref = dx.at[spot(s, c)]
-        return pltpu.make_async_remote_copy(ref, ref, s_gs, s_gr, (dp, sib), MESH)
+        ref = dx.at[spot(s)]
+        return remote(ref, ref, s_gs, s_gr, sib)
+
+    def both(a, b):
+        return pl.when(jnp.logical_and(a, b))
 
     def serve_a(k):
-        to_sib(k).wait_recv()
-        b, n = div(k, NC), rem(k, NC)
-        total = own[k] + dx[ds(b, RB), ds(c * NC + n, CB)].astype(F32)
-
-        @pl.when(edge)
+        @pl.when(adds)
+        def _():
+            to_sib(k).wait_recv()
+
+        def total(h):
+            rows, cols = spot(k * SUB + h)
+            return own[rem(k, DEPTH), pl.ds(h * PR_ROWS, PR_ROWS), :] + dx[rows, cols].astype(F32)
+
+        @both(adds, edge)
         def _():
             for h in range(SUB):
                 s = k * SUB + h
-                tb[s] = total[h * PR_ROWS : (h + 1) * PR_ROWS].astype(BF16)
+                tb[s] = total(h).astype(BF16)
+                to_mid(s).start()
+
+        @both(adds, mid)
+        def _():
             for h in range(SUB):
-                to_mid(k * SUB + h).start()
-
-        @pl.when(mid)
-        def _():
-            own[k] = total
+                own[rem(k, DEPTH), pl.ds(h * PR_ROWS, PR_ROWS), :] = total(h)
 
     def serve_p(s):
-        @pl.when(mid)
+        @both(adds, mid)
         def _():
             to_mid(s).wait_recv()
             k, h = div(s, SUB), rem(s, SUB)
-            tb[s] = (own[k, ds(h, PR_ROWS), :] + tb[s].astype(F32)).astype(BF16)
+            tb[s] = (own[rem(k, DEPTH), ds(h, PR_ROWS), :] + tb[s].astype(F32)).astype(BF16)
             to_across(s).start()
+            part_to_sib(s).start()
 
     def serve_f(s):
-        @pl.when(mid)
-        def _():
+        @both(ends, mid)
+        def _():
+            part_to_sib(s).wait_recv()
             to_across(s).wait_recv()
-            dx[spot(s, c)] = (tb[s].astype(F32) + pr[s].astype(F32)).astype(BF16)
+            rows, cols = spot(s)
+            dx[rows, cols] = (dx[rows, cols].astype(F32) + tb[s].astype(F32)).astype(BF16)
             to_edge(s).start()
             final_to_sib(s).start()
 
     def serve_g(s):
-        @pl.when(edge)
+        @both(ends, edge)
         def _():
             to_edge(s).wait_recv()
             final_to_sib(s).start()
@@ -212,22 +226,23 @@
 
     def step1(i, _):
         b, n = div(i, NC), rem(i, NC)
-        qs, qo = (1 - c) * NC + n, c * NC + n
 
         @pl.when(b == 0)
         def _():
-            for q in (qs, qo):
-                load_wg(q).wait()
-                load_wu(q).wait()
-
-        @pl.when(i >= SLOTS)
+            load_wg(n).wait()
+            load_wu(n).wait()
+
+        @both(ends, i >= SLOTS)
         def _():
             to_sib(i - SLOTS).wait_send()
 
-        theirs, ours = term(b, qs), term(b, qo)
-        stage[rem(i, SLOTS)] = theirs.astype(BF16)
-        own[i] = ours
-        to_sib(i).start()
+        t = term(i)
+        own[rem(i, DEPTH)] = t
+        stage[rem(i, SLOTS)] = t.astype(BF16)
+
+        @pl.when(ends)
+        def _():
+            to_sib(i).start()
 
         @pl.when(i >= 1)
         def _():
@@ -301,21 +316,32 @@
 
     lax.fori_loop(base, PIECES + LAG_G, step4, 0)
 
-    for k in range(SLOTS):
-        to_sib(CHUNKS - SLOTS + k).wait_send()
-    other = dx.at[:, ds(1 - c, HALF)]
-    mine = dx.at[:, ds(c, HALF)]
-    pltpu.make_async_copy(tb, tb, s_t).wait()
-    pltpu.make_async_copy(mine, mine, s_gs).wait()
-    pltpu.make_async_copy(other, other, s_gr).wait()
-
-    @pl.when(mid)
-    def _():
-        pltpu.make_async_copy(mine, mine, s_f).wait()
+    @pl.when(adds)
+    def _():
+        pltpu.make_async_copy(tb, tb, s_t).wait()
+        pltpu.make_async_copy(dx, dx, s_gr).wait()
+
+    @both(adds, mid)
+    def _():
+        pltpu.make_async_copy(tb, tb, s_gs).wait()
+
+    @pl.when(ends)
+    def _():
+        for k in range(SLOTS):
+            to_sib(CHUNKS - SLOTS + k).wait_send()
+        pltpu.make_async_copy(dx, dx, s_gs).wait()
+
+    @both(ends, mid)
+    def _():
+        pltpu.make_async_copy(dx, dx, s_f).wait()
 
 
 def writer(a, b, c, d, oa, ob, oc, od, sems):
-    copies = [pltpu.make_async_copy(s, t, sems.at[i]) for i, (s, t) in enumerate(((a, oa), (b, ob), (c, oc), (d, od)))]
+    copies = []
+    for i, (src, dst) in enumerate(((a, oa), (b, ob), (c, oc), (d, od))):
+        for k in range(4):
+            rows = pl.ds(k * (src.shape[0] // 4), src.shape[0] // 4)
+            copies.append(pltpu.make_async_copy(src.at[rows], dst.at[rows], sems.at[i, k]))
     for copy in copies:
         copy.start()
     for copy in copies:
@@ -336,8 +362,7 @@
                 pltpu.VMEM((ROWS, D), BF16),
                 pltpu.VMEM((ROWS, 2 * FF), BF16),
                 pltpu.VMEM((ROWS, FF), BF16),
-                pltpu.VMEM((CHUNKS, RB, CB), F32),
-                pltpu.VMEM((PIECES, PR_ROWS, CB), BF16),
+                pltpu.VMEM((DEPTH, RB, CB), F32),
                 pltpu.VMEM((PIECES, PR_ROWS, CB), BF16),
                 pltpu.VMEM((SLOTS, RB, CB), BF16),
                 pltpu.VMEM((2, RB, FF), BF16),
@@ -346,7 +371,7 @@
                 dma((NB,)),
                 dma((2,)),
                 dma((2,)),
-                dma((2, 2 * NC)),
+                dma((2, NC)),
                 dma((HP,)),
                 dma((2,)),
                 dma((SLOTS,)),
@@ -367,7 +392,7 @@
             out_shape=[jax.ShapeDtypeStruct(s, BF16) for s in shapes],
             in_specs=[pl.BlockSpec(memory_space=pltpu.VMEM)] * 4,
             out_specs=[pl.BlockSpec(memory_space=pl.ANY)] * 4,
-            scratch_shapes=[pltpu.SemaphoreType.DMA((4,))],
+            scratch_shapes=[pltpu.SemaphoreType.DMA((4, 4))],
             compiler_params=pltpu.CompilerParams(vmem_limit_bytes=1024 * 1024),
         )(*parts)
 

time: 119 us -> 119 us (level)
  no operation moved by 1% of the time
where the time goes in v3:
time: 119 us
  Pallas kernels  118 us (99%)
    pallas_call x1, Pallas kernels, step(): pl.pallas_call(kernel, out_shape=[pltpu.VMEM(s, BF16) for s in shapes], i...  112 us
    pallas_call x1, Pallas kernels, step(): pl.pallas_call(writer, out_shape=[jax.ShapeDtypeStruct(s, BF16) for s in...  6.27 us

profile of v3, /device:TPU:0, one launch (start us, length us, event | category | flops | bytes accessed | tf_op | source)
XLA Modules:
  0.0 118.8 jit_solution(10792450542171625354)
XLA Ops:
  0.6 111.9 %shard_map.102 = (bf16[2048,2048]{1,0:T(8,128)(2,1)S(1)}, bf16[2048,768]{1,0:T(8,128)(2,1)S(1)}, bf16[2048,768]{1,0:T(8,128)(2,1)S(1)}, bf16[768,2048]{1,0:T(8,128)(2,1)S(1)}) custom-call(bf16[2048,2048]{1,0:T(8,128)(2,1)} %x.1, bf16[2048,2048]{1,0:T(8,128)(2,1)} %dy.1, bf16[2048,768]{1,0:T(8,128)(2,1)} %gate.1, bf16[2048,768]{1,0:T(8,128)(2,1)} %up.1, ...), custom_call_target="tpu_custom_call" | custom-call | tf_op jit(solution)/shard_map/pallas_call | solution.py:356
  112.6 6.3 %shard_map.103 = (bf16[2048,2048]{1,0:T(8,128)(2,1)}, bf16[2048,768]{1,0:T(8,128)(2,1)}, bf16[2048,768]{1,0:T(8,128)(2,1)}, bf16[768,2048]{1,0:T(8,128)(2,1)}) custom-call(bf16[2048,2048]{1,0:T(8,128)(2,1)S(1)} %get-tuple-element.8.a, bf16[2048,768]{1,0:T(8,128)(2,1)S(1)} %get-tuple-element.9.b, bf16[2048,768]{1,0:T(8,128)(2,1)S(1)} %get-tuple-element.10.c, ...), custom_call_target="tpu_custom_call" | custom-call | tf_op jit(solution)/shard_map/pallas_call | solution.py:390

commit v4 on v3

--- a/solution.py
+++ b/solution.py
@@ -22,7 +22,7 @@
 SLOTS = 4
 DEPTH = 16
 HP = FF // 256
-LAG_P, LAG_F, LAG_G = 4, 8, 12
+LAG_P, LAG_F, LAG_G = 5, 9, 14
 PER_BLOCK = NC + 1
 
 NT = (((1,), (1,)), ((), ()))

time: 119 us -> 119 us (level)
  no operation moved by 1% of the time
where the time goes in v4:
time: 119 us
  Pallas kernels  118 us (99%)
    pallas_call x1, Pallas kernels, step(): pl.pallas_call(kernel, out_shape=[pltpu.VMEM(s, BF16) for s in shapes], i...  112 us
    pallas_call x1, Pallas kernels, step(): pl.pallas_call(writer, out_shape=[jax.ShapeDtypeStruct(s, BF16) for s in...  6.27 us

profile of v4, /device:TPU:0, one launch (start us, length us, event | category | flops | bytes accessed | tf_op | source)
XLA Modules:
  0.0 118.8 jit_solution(6135373026024024795)
XLA Ops:
  0.6 111.9 %shard_map.102 = (bf16[2048,2048]{1,0:T(8,128)(2,1)S(1)}, bf16[2048,768]{1,0:T(8,128)(2,1)S(1)}, bf16[2048,768]{1,0:T(8,128)(2,1)S(1)}, bf16[768,2048]{1,0:T(8,128)(2,1)S(1)}) custom-call(bf16[2048,2048]{1,0:T(8,128)(2,1)} %x.1, bf16[2048,2048]{1,0:T(8,128)(2,1)} %dy.1, bf16[2048,768]{1,0:T(8,128)(2,1)} %gate.1, bf16[2048,768]{1,0:T(8,128)(2,1)} %up.1, ...), custom_call_target="tpu_custom_call" | custom-call | tf_op jit(solution)/shard_map/pallas_call | solution.py:356
  112.6 6.3 %shard_map.103 = (bf16[2048,2048]{1,0:T(8,128)(2,1)}, bf16[2048,768]{1,0:T(8,128)(2,1)}, bf16[2048,768]{1,0:T(8,128)(2,1)}, bf16[768,2048]{1,0:T(8,128)(2,1)}) custom-call(bf16[2048,2048]{1,0:T(8,128)(2,1)S(1)} %get-tuple-element.8.a, bf16[2048,768]{1,0:T(8,128)(2,1)S(1)} %get-tuple-element.9.b, bf16[2048,768]{1,0:T(8,128)(2,1)S(1)} %get-tuple-element.10.c, ...), custom_call_target="tpu_custom_call" | custom-call | tf_op jit(solution)/shard_map/pallas_call | solution.py:390
